TPU v7x, 32 devices: a whole 2x2x4 slice. The times are simulated.
32 devices in a mesh: dp: 8 (over z, y), tp: 4 (over x, core).
Axes of the slice: x: 2, y: 2, z: 4, core: 2. Of those that a mesh axis runs over, the one named last changes fastest.
Arguments:
- queries: bfloat16 [2048, 4096], P('dp', 'tp'), may hold values from -6 to 6
- keys: bfloat16 [2048, 512], P(('dp', 'tp')), may hold values from -6 to 6
- values: bfloat16 [2048, 512], P(('dp', 'tp')), may hold values from -6 to 6
- out_weight: bfloat16 [4096, 8192], P('tp', 'dp'), may hold values from -0.09375 to 0.09375
- residual: bfloat16 [2048, 8192], P(('dp', 'tp')), may hold values from -40 to 40
- norm_gain: float32 [8192], replicated, may hold values from 0.5 to 1.5
Outputs:
- hidden_out: bfloat16 [2048, 8192], P(('dp', 'tp'))
- normed: bfloat16 [2048, 8192], P(('dp', 'tp'))
All inputs are finite; a program needn't handle non-finite values.
Results may differ from a plain program's by a relative error of at most 0.012.
Values may be sent and summed in bfloat16 or wider, within the bound.
No kernel may reach another device: no remote copies, remote signals or barrier semaphores. Data moves between devices by JAX's collectives and lax.ppermute only.
A program may use at most 64 MiB of HBM per device.

v0:
```python
import math

import jax
import jax.numpy as jnp
from jax import lax
from jax.sharding import PartitionSpec as P

KVH = 4
HDIM = 128
LEN = 32


def attention(queries, key_head, value_head):
    rows = queries.shape[0]
    sequences = rows // LEN
    local_heads = queries.shape[1] // HDIM
    query_heads = queries.reshape(sequences, LEN, local_heads, HDIM)
    key_rows = key_head.reshape(sequences, LEN, HDIM)
    value_rows = value_head.reshape(sequences, LEN, HDIM)
    scores = jnp.einsum(
        "slhd,smd->shlm", query_heads, key_rows, preferred_element_type=jnp.float32
    ) / math.sqrt(HDIM)
    causal = jnp.arange(LEN)[:, None] >= jnp.arange(LEN)[None, :]
    scores = jnp.where(causal, scores, -1e30)
    highest = jnp.max(scores, axis=-1, keepdims=True)
    powers = jnp.exp(scores - highest)
    weights = (powers / jnp.sum(powers, axis=-1, keepdims=True)).astype(jnp.bfloat16)
    attended = jnp.einsum("shlm,smd->slhd", weights, value_rows, preferred_element_type=jnp.float32)
    return attended.astype(jnp.bfloat16).reshape(rows, local_heads * HDIM)


def local(queries, keys, values, out_weight, residual, norm_gain):
    tp_size = lax.axis_size("tp")
    position = lax.axis_index("tp")
    gathered_keys, gathered_values = (
        lax.all_gather(keys, "tp", axis=0, tiled=True),
        lax.all_gather(values, "tp", axis=0, tiled=True),
    )
    head = position * KVH // tp_size
    key_head = lax.dynamic_slice_in_dim(gathered_keys, head * HDIM, HDIM, 1)
    value_head = lax.dynamic_slice_in_dim(gathered_values, head * HDIM, HDIM, 1)
    attended = attention(queries, key_head, value_head)
    partial_value = jnp.dot(
        attended,
        lax.all_gather(out_weight, "dp", axis=1, tiled=True),
        preferred_element_type=jnp.float32,
    )
    projected = lax.psum_scatter(
        partial_value.astype(jnp.bfloat16), "tp", scatter_dimension=0, tiled=True
    ).astype(jnp.float32)
    updated = residual.astype(jnp.float32) + projected
    hidden_out = updated.astype(jnp.bfloat16)
    meansq = jnp.mean(updated * updated, axis=-1, keepdims=True)
    normed = (updated * lax.rsqrt(meansq + 1e-05) * norm_gain).astype(jnp.bfloat16)
    return (hidden_out, normed)


def solution(mesh):
    return jax.shard_map(
        local,
        mesh=mesh,
        in_specs=(
            P("dp", "tp"),
            P(("dp", "tp"), None),
            P(("dp", "tp"), None),
            P("tp", "dp"),
            P(("dp", "tp"), None),
            P(),
        ),
        out_specs=(P(("dp", "tp"), None), P(("dp", "tp"), None)),
        check_vma=False,
    )
```

profile of v0, /device:TPU:0, one launch (start us, length us, event | category | flops | bytes accessed | tf_op | source)
XLA Modules:
  0.0 305.3 jit_solution(16371543206600074251)
XLA Ops:
  7.2 0.0 copy-start.2
  7.2 0.0 copy-start.3
  7.2 0.0 copy-start.4
  7.2 0.0 all-gather.2.cloned.1.call-start
  7.2 0.7 all-gather.2.cloned.1.call-update
  7.9 0.0 reduce-scatter.2.cloned.1.call-start
  8.0 0.2 copy-done.2
  8.2 0.1 copy.16
  8.3 0.0 copy-done.3
  8.3 7.2 %all_gather.10 = bf16[256,512]{1,0:T(8,128)(2,1)S(1)} all-gather(bf16[64,512]{1,0:T(8,128)(2,1)S(1)} %copy-done.3), channel_id=1, replica_groups=mesh['dp'=8,'tp'=4] {'tp'}, dimensions={0}, use_global_device_ids=true | all-gather | bytes 327680 | tf_op jit(solution)/shard_map/all_gather | solution.py:36
  15.5 0.0 copy-done.4
  15.5 5.8 %all_gather.9 = bf16[256,512]{1,0:T(8,128)(2,1)S(1)} all-gather(bf16[64,512]{1,0:T(8,128)(2,1)S(1)} %copy-done.4), channel_id=1, replica_groups=mesh['dp'=8,'tp'=4] {'tp'}, dimensions={0}, use_global_device_ids=true | all-gather | bytes 327680 | tf_op jit(solution)/shard_map/all_gather | solution.py:37
  21.4 1.0 fusion.15
  22.4 0.9 fusion.5
  23.3 0.5 fusion.6
  23.8 0.2 copy.12
  24.0 216.2 %all-gather.2.cloned.1.call-done = bf16[1024,8192]{1,0:T(8,128)(2,1)} async-done(((bf16[1024,1024]{1,0:T(8,128)(2,1)}), bf16[1024,8192]{1,0:T(8,128)(2,1)}) %all-gather.2.cloned.1.call-update) | async-done | bytes 16777232 | tf_op jit(solution)/shard_map/all_gather | solution.py:45
  240.2 11.8 %convolution_convert_fusion = bf16[256,8192]{1,0:T(8,128)(2,1)} fusion(bf16[1024,8192]{1,0:T(8,128)(2,1)} %all-gather.2.cloned.1.call-done, bf16[32,8,8,128]{3,2,1,0:T(8,128)(2,1)S(1)} %bitcast.36), kind=kOutput, calls=%fused_computation.1 | convolution fusion | flops 4297064448 | bytes 21495808 | tf_op jit(solution)/shard_map/dot_general | solution.py:43
  252.0 0.0 reduce-scatter.2.cloned.1.call-update
  252.0 0.0 copy-start.5
  252.0 42.9 %reduce-scatter.2.cloned.1.call-done = bf16[64,8192]{1,0:T(8,128)(2,1)} async-done(((bf16[256,8192]{1,0:T(8,128)(2,1)}), bf16[64,8192]{1,0:T(8,128)(2,1)}) %reduce-scatter.2.cloned.1.call-update) | async-done | bytes 1048592 | tf_op jit(solution)/shard_map/reduce_scatter | solution.py:48
  294.9 0.0 copy-done
  294.9 1.8 multiply_reduce_fusion
  296.7 1.8 multiply_convert_fusion
  (8 shorter events, 0.0 us)
Async XLA Ops:
  7.2 1.0 copy-start.2
  7.2 1.1 copy-start.3
  7.2 8.4 %copy-start.4 = (bf16[64,512]{1,0:T(8,128)(2,1)S(1)}, bf16[64,512]{1,0:T(8,128)(2,1)}, u32[]{:S(2)}) copy-start(bf16[64,512]{1,0:T(8,128)(2,1)} %param.8) | copy-start | bytes 196612
  7.2 233.0 %all-gather.2.cloned.1.call-start = ((), (), s32[]{:S(2)}) async-start(), calls=%async_computation.1 | async-start | bytes 18874368 | tf_op jit(solution)/shard_map/all_gather | solution.py:45
  7.9 287.0 %reduce-scatter.2.cloned.1.call-start = ((), (), s32[]{:S(2)}) async-start(), calls=%async_computation.2 | async-start | bytes 5242880 | tf_op jit(solution)/shard_map/reduce_scatter | solution.py:48
  252.0 42.9 %copy-start = (bf16[64,8192]{1,0:T(8,128)(2,1)S(1)}, bf16[64,8192]{1,0:T(8,128)(2,1)}, u32[]{:S(2)}) copy-start(bf16[64,8192]{1,0:T(8,128)(2,1)} %param.10) | copy-start | bytes 3145732
  252.0 44.7 %copy-start.5 = (f32[8192]{0:T(1024)S(1)}, f32[8192]{0:T(1024)}, u32[]{:S(2)}) copy-start(f32[8192]{0:T(1024)} %param.11) | copy-start | bytes 98308
  294.9 1.8 copy-start.1
Sparse Core Ops, SparseCore 0:
  10.2 229.9 all-gather.1
  252.1 42.7 reduce-scatter.1
where the time goes:
time: 306 us; the launch traced here: 305 us
  waiting for transfers between devices  260 us (85%)
  between operations  14.2 us (5%)
  matrix products  14.1 us (5%)
  blocking collectives  13.1 us (4%)
  other arithmetic  3.53 us (1%)
    all_gather x1, waiting for transfers between devices, local(): lax.all_gather(out_weight, 'dp', axis=1, tiled=True)  216 us
    reduce_scatter x1, waiting for transfers between devices, local(): lax.psum_scatter(partial_value.astype(jnp.bfloat16), 'tp', scatter_dimens...  42.9 us
    dot_general x1, matrix products, local(): jnp.dot(attended, lax.all_gather(out_weight, 'dp', axis=1, tiled=True), p...  11.8 us
    all_gather x1, blocking collectives, local(): lax.all_gather(keys, 'tp', axis=0, tiled=True)  7.22 us
  transfers between devices with their start and end apart: 2, of which 2 were waited for; matrix products, arithmetic and copies ran while one was open for 1% of the time, Pallas kernels for 0%

commit v1 on v0

v1 whole, which is shorter than its diff:
```python
import functools
import math

import jax
import jax.numpy as jnp
from jax import lax
from jax.experimental import pallas as pl
from jax.experimental.pallas import tpu as pltpu
from jax.sharding import PartitionSpec as P


KVH = 4
HDIM = 128
LEN = 32
STEPS = 4
VMEM = pl.BlockSpec(memory_space=pltpu.VMEM)
PARAMS = pltpu.CompilerParams(vmem_limit_bytes=16 * 1024 * 1024)


def tp_place():
    at = lax.axis_index("tp")
    return at // 2, at % 2, lax.axis_size("tp") // 2


def turns(n_far):
    return [(k, flip) for k in range(n_far) for flip in ((0, 1) if k == 0 else (1, 0))]


def share(keys_ref, values_ref, *block_refs):
    far, near, n_far = tp_place()
    for (k, flip), block_ref in zip(turns(n_far), block_refs):
        target = (far + k) % n_far * 2 + (near + flip) % 2
        head = target * KVH // (2 * n_far)
        lanes = pl.ds(pl.multiple_of(head * HDIM, HDIM), HDIM)
        block_ref[:, :HDIM] = keys_ref[:, lanes]
        block_ref[:, HDIM:] = values_ref[:, lanes]


def gather(*refs):
    *block_refs, held_ref = refs
    far, near, n_far = tp_place()
    rows = block_refs[0].shape[0]
    for (k, flip), block_ref in zip(turns(n_far), block_refs):
        source = (far + n_far - k) % n_far * 2 + (near + flip) % 2
        held_ref[pl.ds(pl.multiple_of(source * rows, rows), rows), :] = block_ref[...]


def attend(rows, queries_ref, held_ref, out_ref):
    far, near, n_far = tp_place()
    tokens = held_ref.shape[0]
    group = min(tokens, 4 * LEN)
    heads = queries_ref.shape[1] // HDIM
    at_query = lax.broadcasted_iota(jnp.int32, (group, group), 0)
    at_key = lax.broadcasted_iota(jnp.int32, (group, group), 1)
    seen = (at_query // LEN == at_key // LEN) & (at_query >= at_key)
    for first in range(0, tokens, group):
        queries = jnp.concatenate(
            [queries_ref[first : first + group, h * HDIM : (h + 1) * HDIM] for h in range(heads)],
            axis=0,
        )
        scores = lax.dot_general(
            queries,
            held_ref[first : first + group, :HDIM],
            (((1,), (1,)), ((), ())),
            preferred_element_type=jnp.float32,
        ) * (1 / math.sqrt(HDIM))
        scores = jnp.where(seen[None], scores.reshape(heads, group, group), -1e30)
        powers = jnp.exp(scores - jnp.max(scores, axis=-1, keepdims=True))
        powers = powers.astype(jnp.bfloat16).reshape(heads * group, group)
        values = jnp.concatenate(
            [held_ref[first : first + group, HDIM:], jnp.ones((group, HDIM), jnp.bfloat16)], axis=1
        )
        attended = jnp.dot(powers, values, preferred_element_type=jnp.float32)
        attended = (attended[:, :HDIM] / attended[:, HDIM:]).astype(jnp.bfloat16)
        for start in range(0, group, rows):
            device = (first + start) // rows
            place = (device // 2 + n_far - far) % n_far + (near + device + 1) % 2 * n_far
            at = pl.ds(pl.multiple_of(place * rows, rows), rows)
            for head in range(heads):
                block = head * group + start
                out_ref[at, head * HDIM : (head + 1) * HDIM] = attended[block : block + rows]


def project(products, n_chunks, *refs):
    *sources, sent_ref, kept_ref = refs
    chunks, pieces = sources[:n_chunks], sources[n_chunks:]
    half, start = sent_ref.shape[0], 0
    for chunk, piece in products:
        width = pieces[piece].shape[1]
        step = math.gcd(width, 512)
        for at in range(0, width, step):
            total = jnp.dot(
                chunks[chunk][...],
                pieces[piece][:, at : at + step],
                preferred_element_type=jnp.float32,
            )
            lanes = slice(start + at, start + at + step)
            sent_ref[:, lanes] = total[:half].astype(jnp.bfloat16)
            kept_ref[:, lanes] = total[half:]
        start += width


def finish(n_inner, unit, slots, residual_ref, gain_ref, *refs):
    pieces = refs[: len(slots)]
    hidden_ref, normed_ref, updated_ref = refs[len(slots) :]
    at = lax.axis_index("dp")
    outer, inner = at // n_inner, at % n_inner
    split = residual_ref.shape[1] // (unit * lax.axis_size("dp"))
    total = jnp.zeros((residual_ref.shape[0], 1), jnp.float32)
    for piece, owned in zip(pieces, slots):
        for place, (j, k, part) in enumerate(owned):
            column = ((outer ^ j) * n_inner + (inner + k) % n_inner) * split + part
            at = pl.ds(pl.multiple_of(column * unit, unit), unit)
            block = piece[:, place * unit : (place + 1) * unit].astype(jnp.float32)
            updated = residual_ref[:, at].astype(jnp.float32) + block
            updated_ref[:, at] = updated
            hidden_ref[:, at] = updated.astype(jnp.bfloat16)
            total += jnp.sum(updated * updated, axis=-1, keepdims=True)
    scale = lax.rsqrt(total / residual_ref.shape[1] + 1e-05)
    for slot in range(residual_ref.shape[1] // unit):
        at = pl.ds(slot * unit, unit)
        normed_ref[:, at] = (updated_ref[:, at] * scale * gain_ref[:, at]).astype(jnp.bfloat16)


def local(queries, keys, values, out_weight, residual, norm_gain):
    tp_size, dp_size = lax.axis_size("tp"), lax.axis_size("dp")
    n_outer, n_far = math.gcd(dp_size, STEPS), tp_size // 2
    n_inner = dp_size // n_outer
    rows, width = keys.shape[0], out_weight.shape[1]
    split = 2 if n_inner == 2 else 1
    unit = width // split

    def over_inner(value, steps):
        pairs = [
            (o * n_inner + i, o * n_inner + (i + steps) % n_inner)
            for o in range(n_outer)
            for i in range(n_inner)
        ]
        return lax.ppermute(value, "dp", pairs)

    def over_outer(value, pairs):
        every = [(a * n_inner + i, b * n_inner + i) for a, b in pairs for i in range(n_inner)]
        return lax.ppermute(value, "dp", every)

    def crossed(j):
        return [(o, o ^ j) for o in range(n_outer)]

    def over_tp(value, steps, flip):
        pairs = [
            (q * 2 + c, (q + steps) % n_far * 2 + (c ^ flip))
            for q in range(n_far)
            for c in range(2)
        ]
        return lax.ppermute(value, "tp", pairs)

    if n_inner == 2:
        units = [[(0, h) for h in range(split)], [(1, 0)], [(1, 1)]]
    else:
        middle = n_inner // 2 + 1
        units = [[(0, 0)], [(k, 0) for k in range(1, middle)], [(k, 0) for k in range(middle, n_inner)]]
    block_type = jax.ShapeDtypeStruct((rows, 2 * HDIM), jnp.bfloat16)
    blocks = pl.pallas_call(
        share,
        out_shape=[block_type] * tp_size,
        in_specs=[VMEM, VMEM],
        out_specs=[VMEM] * tp_size,
        compiler_params=PARAMS,
        name="share",
    )(keys, values)
    later = lax.optimization_barrier((out_weight, blocks[0]))[0]
    if n_inner == 2:
        weights = [out_weight, over_inner(out_weight[:, :unit], 1), over_inner(later[:, unit:], 1)]
    else:
        weights = [out_weight] + [
            jnp.concatenate([over_inner(out_weight, -k) for k, _ in units[at]], axis=1)
            for at in (1, 2)
        ]
    blocks = [
        over_tp(block, k, flip) if k or flip else block
        for (k, flip), block in zip(turns(n_far), blocks)
    ]
    tokens, depth = queries.shape
    chunk_type = jax.ShapeDtypeStruct((tokens, depth), jnp.bfloat16)
    held = pl.pallas_call(
        gather,
        out_shape=jax.ShapeDtypeStruct((tokens, 2 * HDIM), jnp.bfloat16),
        in_specs=[VMEM] * len(blocks),
        out_specs=VMEM,
        compiler_params=PARAMS,
        name="gather",
    )(*blocks)
    own = pl.pallas_call(
        functools.partial(attend, rows),
        out_shape=chunk_type,
        in_specs=[VMEM, VMEM],
        out_specs=VMEM,
        cost_estimate=pl.CostEstimate(
            flops=4 * tokens * depth * 4 * LEN, bytes_accessed=4 * tokens * depth, transcendentals=0
        ),
        compiler_params=PARAMS,
        name="attend",
    )(queries, held)

    chunks = [own]
    if n_outer >= 2:
        chunks.append(over_outer(own, crossed(1)))
    if n_outer == 4:
        chunks.append(over_outer(own, crossed(2)))
        direct = over_outer(own, [(1, 2), (2, 1)])
        relayed = over_outer(chunks[2], [(1, 0), (2, 3)])
        chunks.append(direct + relayed)

    if n_outer == 4:
        events = [
            [(0, 0)],
            [(0, 1), (1, 0), (1, 1)],
            [(2, 0), (2, 1)],
            [(3, 0), (3, 1)],
            [(0, 2), (1, 2), (2, 2), (3, 2)],
        ]
    else:
        events = [[(j, piece) for j in range(n_outer) for piece in range(3)]]

    half = rows * n_far
    landed, slots = [], []
    for products in events:
        used = sorted({j for j, _ in products})
        held = sorted({piece for _, piece in products})
        total_width = sum(weights[piece].shape[1] for _, piece in products)
        sent, kept = pl.pallas_call(
            functools.partial(
                project, [(used.index(j), held.index(p)) for j, p in products], len(used)
            ),
            out_shape=(
                jax.ShapeDtypeStruct((half, total_width), jnp.bfloat16),
                jax.ShapeDtypeStruct((half, total_width), jnp.float32),
            ),
            in_specs=[VMEM] * (len(used) + len(held)),
            out_specs=(VMEM, VMEM),
            cost_estimate=pl.CostEstimate(
                flops=2 * tokens * depth * total_width,
                bytes_accessed=2 * depth * total_width,
                transcendentals=0,
            ),
            compiler_params=PARAMS,
        )(*[chunks[j] for j in used], *[weights[p] for p in held])
        total = kept + over_tp(sent, 0, 1).astype(jnp.float32)
        arrived = [
            over_tp(total[k * rows : (k + 1) * rows].astype(jnp.bfloat16), k, 0)
            for k in range(1, n_far)
        ]
        start = 0
        for j in used:
            pieces = [p for i, p in products if i == j]
            stop = start + sum(weights[p].shape[1] for p in pieces)
            mine = total[:rows, start:stop]
            for other in arrived:
                mine += other[:, start:stop].astype(jnp.float32)
            mine = mine.astype(jnp.bfloat16)
            landed.append(over_outer(mine, crossed(j)) if j else mine)
            slots.append([(j, k, part) for p in pieces for k, part in units[p]])
            start = stop

    shape = jax.ShapeDtypeStruct(residual.shape, jnp.bfloat16)
    return pl.pallas_call(
        functools.partial(finish, n_inner, unit, slots),
        out_shape=(shape, shape),
        in_specs=[VMEM] * (2 + len(landed)),
        out_specs=(VMEM, VMEM),
        scratch_shapes=[pltpu.VMEM(residual.shape, jnp.float32)],
        compiler_params=PARAMS,
        name="finish",
    )(residual, norm_gain.reshape(1, -1), *landed)


def solution(mesh):
    return jax.shard_map(
        local,
        mesh=mesh,
        in_specs=(
            P("dp", "tp"),
            P(("dp", "tp"), None),
            P(("dp", "tp"), None),
            P("tp", "dp"),
            P(("dp", "tp"), None),
            P(),
        ),
        out_specs=(P(("dp", "tp"), None), P(("dp", "tp"), None)),
        check_vma=False,
    )
```

time: 306 us -> 94.1 us (0.31)
  waiting for transfers between devices: 260 us -> 51.2 us
  starting transfers between devices: 0.08 us -> 28.5 us
  matrix products: 14.1 us -> 0 us
  between operations: 14.2 us -> 0.94 us
  blocking collectives: 13.1 us -> 0 us
  Pallas kernels: 0 us -> 7.87 us
  local copies, waits for them, and re-layouts: 0.57 us -> 4.4 us
    all_gather x1 -> x0, waiting for transfers between devices: 216 us -> none  [local(): lax.all_gather(out_weight, 'dp', axis=1, tiled=True)]
    ppermute x0 -> x25, waiting for transfers between devices: none -> 51.2 us  [the longest x10 31.5 us: over_outer(): return lax.ppermute(value, 'dp', every)]
    reduce_scatter x1 -> x0, waiting for transfers between devices: 42.9 us -> none  [local(): lax.psum_scatter(partial_value.astype(jnp.bfloat16), 'tp', scatter_dimens...]
    ppermute x0 -> x25, starting transfers between devices: none -> 28.5 us  [the longest x10 16.7 us: over_outer(): return lax.ppermute(value, 'dp', every)]
    dot_general x3 -> x0, matrix products: 13.2 us -> none  [the longest x1 11.8 us: local(): jnp.dot(attended, lax.all_gather(out_weight, 'dp', axis=1, tiled=True), p...]
    all_gather x2 -> x0, blocking collectives: 13.1 us -> none  [the longest x1 7.22 us: local(): lax.all_gather(keys, 'tp', axis=0, tiled=True)]
    pallas_call x0 -> x9, Pallas kernels: none -> 7.87 us  [the longest x5 5.14 us: local(): pl.pallas_call(functools.partial(project, [(used.index(j), held.index(p))...]
  transfers between devices with their start and end apart: 2 -> 25, of which waited for: 2 -> 14; matrix products, arithmetic and copies ran while one was open for 1% -> 1% of each run, Pallas kernels for 0% -> 7%
where the time goes in v1:
time: 94.1 us; the launch traced here: 93.8 us
  waiting for transfers between devices  51.2 us (54%)
  starting transfers between devices  28.5 us (30%)
  Pallas kernels  7.87 us (8%)
  local copies, waits for them, and re-layouts  4.4 us (5%)
    ppermute x10, waiting for transfers between devices, over_outer(): return lax.ppermute(value, 'dp', every)  31.5 us
    ppermute x13, waiting for transfers between devices, over_tp(): return lax.ppermute(value, 'tp', pairs)  19.7 us
    ppermute x10, starting transfers between devices, over_outer(): return lax.ppermute(value, 'dp', every)  16.7 us
    ppermute x13, starting transfers between devices, over_tp(): return lax.ppermute(value, 'tp', pairs)  8.21 us
    pallas_call x5, Pallas kernels, local(): pl.pallas_call(functools.partial(project, [(used.index(j), held.index(p))...  5.14 us
    ppermute x2, starting transfers between devices, over_inner(): return lax.ppermute(value, 'dp', pairs)  3.63 us
    unnamed x12, local copies, waits for them, and re-layouts  2.73 us
  transfers between devices with their start and end apart: 25, of which 14 were waited for; matrix products, arithmetic and copies ran while one was open for 1% of the time, Pallas kernels for 7%

profile of v1, /device:TPU:0, one launch (start us, length us, event | category | flops | bytes accessed | tf_op | source)
XLA Modules:
  0.0 93.8 jit_solution(14655739026390114309)
XLA Ops:
  0.6 1.4 %slice.73 = bf16[1024,512]{1,0:T(8,128)(2,1)S(1)} slice(bf16[1024,1024]{1,0:T(8,128)(2,1)} %refs_1_.5), slice={[0:1024], [0:512]} | slice | bytes 2097152 | tf_op jit(solution)/shard_map/slice | solution.py:172
  2.1 3.1 %collective-permute-start.6 = (bf16[1024,512]{1,0:T(8,128)(2,1)S(1)}, bf16[1024,512]{1,0:T(8,128)(2,1)S(1)}, u32[]{:S(2)}, u32[]{:S(2)}) collective-permute-start(bf16[1024,512]{1,0:T(8,128)(2,1)S(1)} %slice.73), channel_id=1, source_target_pairs={{0,4},{4,0},{8,12},{12,8},{16,20},{20,16},{24,28},{28,24},{1,5},{5... | collective-permute-start | bytes 3145736 | tf_op jit(solution)/shard_map/ppermute | solution.py:139
  6.9 1.6 %collective-permute-start.1 = (bf16[64,256]{1,0:T(8,128)(2,1)S(1)}, bf16[64,256]{1,0:T(8,128)(2,1)S(1)}, u32[]{:S(2)}, u32[]{:S(2)}) collective-permute-start(bf16[64,256]{1,0:T(8,128)(2,1)S(1)} %get-tuple-element.19), channel_id=1, source_target_pairs={{0,3},{1,2},{2,1},{3,0},{4,7},{5,6},{6,5},{7,4},{8,11},{9,10},{10,... | collective-permute-start | bytes 98312 | tf_op jit(solution)/shard_map/ppermute | solution.py:154
  9.1 1.3 %collective-permute-done.1.refs_2_ = bf16[64,256]{1,0:T(8,128)(2,1)S(1)} collective-permute-done((bf16[64,256]{1,0:T(8,128)(2,1)S(1)}, bf16[64,256]{1,0:T(8,128)(2,1)S(1)}, u32[]{:S(2)}, u32[]{:S(2)}) %collective-permute-start.1) | collective-permute-done | bytes 32800 | tf_op jit(solution)/shard_map/ppermute | solution.py:154
  10.3 2.1 %collective-permute-done.2.refs_3_ = bf16[64,256]{1,0:T(8,128)(2,1)S(1)} collective-permute-done((bf16[64,256]{1,0:T(8,128)(2,1)S(1)}, bf16[64,256]{1,0:T(8,128)(2,1)S(1)}, u32[]{:S(2)}, u32[]{:S(2)}) %collective-permute-start.2) | collective-permute-done | bytes 32800 | tf_op jit(solution)/shard_map/ppermute | solution.py:154
  14.5 2.7 %collective-permute-start.10 = (bf16[256,1024]{1,0:T(8,128)(2,1)S(1)}, bf16[256,1024]{1,0:T(8,128)(2,1)S(1)}, u32[]{:S(2)}, u32[]{:S(2)}) collective-permute-start(bf16[256,1024]{1,0:T(8,128)(2,1)S(1)} %attend.1.refs_0_), channel_id=1, source_target_pairs={{0,16},{4,20},{8,24},{12,28},{16,0},{20,4},{24,8},{28,12},{1,17},{... | collective-permute-start | bytes 1572872 | tf_op jit(solution)/shard_map/ppermute | solution.py:143
  20.1 2.1 %collective-permute-start.5 = (bf16[256,1024]{1,0:T(8,128)(2,1)S(1)}, bf16[256,1024]{1,0:T(8,128)(2,1)S(1)}, u32[]{:S(2)}, u32[]{:S(2)}) collective-permute-start(bf16[256,1024]{1,0:T(8,128)(2,1)S(1)} %attend.1.refs_0_), channel_id=1, source_target_pairs={{0,8},{4,12},{8,0},{12,4},{16,24},{20,28},{24,16},{28,20},{1,9},{5... | collective-permute-start | bytes 1572872 | tf_op jit(solution)/shard_map/ppermute | solution.py:143
  22.2 18.7 %collective-permute-done.10.refs_0_.refs_2_ = bf16[256,1024]{1,0:T(8,128)(2,1)S(1)} collective-permute-done((bf16[256,1024]{1,0:T(8,128)(2,1)S(1)}, bf16[256,1024]{1,0:T(8,128)(2,1)S(1)}, u32[]{:S(2)}, u32[]{:S(2)}) %collective-permute-start.10) | collective-permute-done | bytes 524320 | tf_op jit(solution)/shard_map/ppermute | solution.py:143
  40.9 1.3 %collective-permute-start.15 = (bf16[256,1024]{1,0:T(8,128)(2,1)S(1)}, bf16[256,1024]{1,0:T(8,128)(2,1)S(1)}, u32[]{:S(2)}, u32[]{:S(2)}) collective-permute-start(bf16[256,1024]{1,0:T(8,128)(2,1)S(1)} %collective-permute-done.10.refs_0_.refs_2_), channel_id=1, source_target_pairs={{8,0},{12,4},{16,24},{20,28},{9,1},{13,5},{17,25},{21,29},{10,2},{... | collective-permute-start | bytes 1572872 | tf_op jit(solution)/shard_map/ppermute | solution.py:143
  44.3 3.0 %collective-permute-done.4 = bf16[64,1024]{1,0:T(8,128)(2,1)S(1)} collective-permute-done((bf16[64,1024]{1,0:T(8,128)(2,1)S(1)}, bf16[64,1024]{1,0:T(8,128)(2,1)S(1)}, u32[]{:S(2)}, u32[]{:S(2)}) %collective-permute-start.4) | collective-permute-done | bytes 131104 | tf_op jit(solution)/shard_map/ppermute | solution.py:154
  47.4 1.2 %shard_map.78 = (bf16[128,2048]{1,0:T(8,128)(2,1)S(1)}, f32[128,2048]{1,0:T(8,128)S(1)}) custom-call(bf16[256,1024]{1,0:T(8,128)(2,1)S(1)} %attend.1.refs_0_, bf16[256,1024]{1,0:T(8,128)(2,1)S(1)} %collective-permute-done.5.refs_1_, bf16[1024,1024]{1,0:T(8,128)(2,1)S(1)} %copy-done, bf16[1024,512]{1,0:T(8,128)(2,1)S(1)} %collective-permute-done.6.refs_3_.refs_2_), custom_call_target="tpu_custom_call" | custom-call | flops 1073741824 | bytes 4194304 | tf_op jit(solution)/shard_map/pallas_call | solution.py:230
  49.2 6.9 %collective-permute-done.15 = bf16[256,1024]{1,0:T(8,128)(2,1)S(1)} collective-permute-done((bf16[256,1024]{1,0:T(8,128)(2,1)S(1)}, bf16[256,1024]{1,0:T(8,128)(2,1)S(1)}, u32[]{:S(2)}, u32[]{:S(2)}) %collective-permute-start.15) | collective-permute-done | bytes 524320 | tf_op jit(solution)/shard_map/ppermute | solution.py:143
  56.4 1.2 %shard_map.81 = (bf16[128,2048]{1,0:T(8,128)(2,1)S(1)}, f32[128,2048]{1,0:T(8,128)S(1)}) custom-call(bf16[256,1024]{1,0:T(8,128)(2,1)S(1)} %attend.1.refs_0_, bf16[256,1024]{1,0:T(8,128)(2,1)S(1)} %collective-permute-done.5.refs_1_, bf16[256,1024]{1,0:T(8,128)(2,1)S(1)} %collective-permute-done.10.refs_0_.refs_2_, ...), custom_call_target="tpu_custom_call" | custom-call | flops 1073741824 | bytes 4194304 | tf_op jit(solution)/shard_map/pallas_call | solution.py:230
  64.1 3.1 %collective-permute-done.12 = bf16[64,1536]{1,0:T(8,128)(2,1)S(1)} collective-permute-done((bf16[64,1536]{1,0:T(8,128)(2,1)S(1)}, bf16[64,1536]{1,0:T(8,128)(2,1)S(1)}, u32[]{:S(2)}, u32[]{:S(2)}) %collective-permute-start.12) | collective-permute-done | bytes 196640 | tf_op jit(solution)/shard_map/ppermute | solution.py:154
  67.2 1.8 %collective-permute-start.13 = (bf16[64,1536]{1,0:T(8,128)(2,1)S(1)}, bf16[64,1536]{1,0:T(8,128)(2,1)S(1)}, u32[]{:S(2)}, u32[]{:S(2)}) collective-permute-start(bf16[64,1536]{1,0:T(8,128)(2,1)S(1)} %fusion.1), channel_id=1, source_target_pairs={{0,16},{4,20},{8,24},{12,28},{16,0},{20,4},{24,8},{28,12},{1,17},{... | collective-permute-start | bytes 589832 | tf_op jit(solution)/shard_map/ppermute | solution.py:143
  69.0 2.4 %collective-permute-done.17 = bf16[64,1536]{1,0:T(8,128)(2,1)S(1)} collective-permute-done((bf16[64,1536]{1,0:T(8,128)(2,1)S(1)}, bf16[64,1536]{1,0:T(8,128)(2,1)S(1)}, u32[]{:S(2)}, u32[]{:S(2)}) %collective-permute-start.17) | collective-permute-done | bytes 196640 | tf_op jit(solution)/shard_map/ppermute | solution.py:154
  71.4 3.7 %collective-permute-start.18 = (bf16[64,1536]{1,0:T(8,128)(2,1)S(1)}, bf16[64,1536]{1,0:T(8,128)(2,1)S(1)}, u32[]{:S(2)}, u32[]{:S(2)}) collective-permute-start(bf16[64,1536]{1,0:T(8,128)(2,1)S(1)} %fusion), channel_id=1, source_target_pairs={{0,24},{4,28},{8,16},{12,20},{16,8},{20,12},{24,0},{28,4},{1,25},{... | collective-permute-start | bytes 589832 | tf_op jit(solution)/shard_map/ppermute | solution.py:143
  75.1 1.9 %collective-permute-done.8 = bf16[64,2048]{1,0:T(8,128)(2,1)S(1)} collective-permute-done((bf16[64,2048]{1,0:T(8,128)(2,1)S(1)}, bf16[64,2048]{1,0:T(8,128)(2,1)S(1)}, u32[]{:S(2)}, u32[]{:S(2)}) %collective-permute-start.8) | collective-permute-done | bytes 262176 | tf_op jit(solution)/shard_map/ppermute | solution.py:154
  77.1 4.6 %collective-permute-done.21 = bf16[64,2048]{1,0:T(8,128)(2,1)S(1)} collective-permute-done((bf16[64,2048]{1,0:T(8,128)(2,1)S(1)}, bf16[64,2048]{1,0:T(8,128)(2,1)S(1)}, u32[]{:S(2)}, u32[]{:S(2)}) %collective-permute-start.21) | collective-permute-done | bytes 262176 | tf_op jit(solution)/shard_map/ppermute | solution.py:154
  81.8 4.2 %collective-permute-start.23 = (bf16[64,512]{1,0:T(8,128)(2,1)S(1)}, bf16[64,512]{1,0:T(8,128)(2,1)S(1)}, u32[]{:S(2)}, u32[]{:S(2)}) collective-permute-start(bf16[64,512]{1,0:T(8,128)(2,1)S(1)} %get-tuple-element.33), channel_id=1, source_target_pairs={{0,16},{4,20},{8,24},{12,28},{16,0},{20,4},{24,8},{28,12},{1,17},{... | collective-permute-start | bytes 196616 | tf_op jit(solution)/shard_map/ppermute | solution.py:143
  86.2 1.8 %collective-permute-done.22.refs_6_ = bf16[64,512]{1,0:T(8,128)(2,1)S(1)} collective-permute-done((bf16[64,512]{1,0:T(8,128)(2,1)S(1)}, bf16[64,512]{1,0:T(8,128)(2,1)S(1)}, u32[]{:S(2)}, u32[]{:S(2)}) %collective-permute-start.22) | collective-permute-done | bytes 65568 | tf_op jit(solution)/shard_map/ppermute | solution.py:143
  88.1 2.0 %collective-permute-done.23.refs_7_ = bf16[64,512]{1,0:T(8,128)(2,1)S(1)} collective-permute-done((bf16[64,512]{1,0:T(8,128)(2,1)S(1)}, bf16[64,512]{1,0:T(8,128)(2,1)S(1)}, u32[]{:S(2)}, u32[]{:S(2)}) %collective-permute-start.23) | collective-permute-done | bytes 65568 | tf_op jit(solution)/shard_map/ppermute | solution.py:143
  90.1 2.0 %collective-permute-done.24.refs_8_ = bf16[64,512]{1,0:T(8,128)(2,1)S(1)} collective-permute-done((bf16[64,512]{1,0:T(8,128)(2,1)S(1)}, bf16[64,512]{1,0:T(8,128)(2,1)S(1)}, u32[]{:S(2)}, u32[]{:S(2)}) %collective-permute-start.24) | collective-permute-done | bytes 65568 | tf_op jit(solution)/shard_map/ppermute | solution.py:143
  92.1 1.7 %finish.1 = (bf16[64,8192]{1,0:T(8,128)(2,1)}, bf16[64,8192]{1,0:T(8,128)(2,1)}) custom-call(bf16[64,8192]{1,0:T(8,128)(2,1)S(1)} %copy-done.1, f32[1,8192]{1,0:T(1,128)S(1)} %bitcast.1, bf16[64,1024]{1,0:T(8,128)(2,1)S(1)} %fusion.3.refs_0_, bf16[64,512]{1,0:T(8,128)(2,1)S(1)} %fusion.8.refs_1_, bf16[64,1536]{1,0:T(8,128)(2,1)S(1)} %collective-permute-done.9.refs_2_, ...), custom_call_target="tpu_custom_call" | custom-call | tf_op jit(solution)/shard_map/finish/pallas_call | solution.py:265
  (66 shorter events, 17.2 us)
Async XLA Ops:
  2.1 40.2 %collective-permute-start.6 = (bf16[1024,512]{1,0:T(8,128)(2,1)S(1)}, bf16[1024,512]{1,0:T(8,128)(2,1)S(1)}, u32[]{:S(2)}, u32[]{:S(2)}) collective-permute-start(bf16[1024,512]{1,0:T(8,128)(2,1)S(1)} %slice.73), channel_id=1, source_target_pairs={{0,4},{4,0},{8,12},{12,8},{16,20},{20,16},{24,28},{28,24},{1,5},{5... | collective-permute-start | bytes 3145736 | tf_op jit(solution)/shard_map/ppermute | solution.py:139
  6.9 2.2 %collective-permute-start = (bf16[64,256]{1,0:T(8,128)(2,1)S(1)}, bf16[64,256]{1,0:T(8,128)(2,1)S(1)}, u32[]{:S(2)}, u32[]{:S(2)}) collective-permute-start(bf16[64,256]{1,0:T(8,128)(2,1)S(1)} %get-tuple-element.18), channel_id=1, source_target_pairs={{0,1},{1,0},{2,3},{3,2},{4,5},{5,4},{6,7},{7,6},{8,9},{9,8},{10,11... | collective-permute-start | bytes 98312 | tf_op jit(solution)/shard_map/ppermute | solution.py:154
  6.9 3.4 %collective-permute-start.1 = (bf16[64,256]{1,0:T(8,128)(2,1)S(1)}, bf16[64,256]{1,0:T(8,128)(2,1)S(1)}, u32[]{:S(2)}, u32[]{:S(2)}) collective-permute-start(bf16[64,256]{1,0:T(8,128)(2,1)S(1)} %get-tuple-element.19), channel_id=1, source_target_pairs={{0,3},{1,2},{2,1},{3,0},{4,7},{5,6},{6,5},{7,4},{8,11},{9,10},{10,... | collective-permute-start | bytes 98312 | tf_op jit(solution)/shard_map/ppermute | solution.py:154
  8.5 3.9 %collective-permute-start.2 = (bf16[64,256]{1,0:T(8,128)(2,1)S(1)}, bf16[64,256]{1,0:T(8,128)(2,1)S(1)}, u32[]{:S(2)}, u32[]{:S(2)}) collective-permute-start(bf16[64,256]{1,0:T(8,128)(2,1)S(1)} %get-tuple-element.20), channel_id=1, source_target_pairs={{0,2},{1,3},{2,0},{3,1},{4,6},{5,7},{6,4},{7,5},{8,10},{9,11},{10,... | collective-permute-start | bytes 98312 | tf_op jit(solution)/shard_map/ppermute | solution.py:154
  14.5 26.4 %collective-permute-start.10 = (bf16[256,1024]{1,0:T(8,128)(2,1)S(1)}, bf16[256,1024]{1,0:T(8,128)(2,1)S(1)}, u32[]{:S(2)}, u32[]{:S(2)}) collective-permute-start(bf16[256,1024]{1,0:T(8,128)(2,1)S(1)} %attend.1.refs_0_), channel_id=1, source_target_pairs={{0,16},{4,20},{8,24},{12,28},{16,0},{20,4},{24,8},{28,12},{1,17},{... | collective-permute-start | bytes 1572872 | tf_op jit(solution)/shard_map/ppermute | solution.py:143
  17.3 39.1 %collective-permute-start.19 = (bf16[1024,512]{1,0:T(8,128)(2,1)S(1)}, bf16[1024,512]{1,0:T(8,128)(2,1)S(1)}, u32[]{:S(2)}, u32[]{:S(2)}) collective-permute-start(bf16[1024,512]{1,0:T(8,128)(2,1)S(1)} %slice.83), channel_id=1, source_target_pairs={{0,4},{4,0},{8,12},{12,8},{16,20},{20,16},{24,28},{28,24},{1,5},{5... | collective-permute-start | bytes 3145736 | tf_op jit(solution)/shard_map/ppermute | solution.py:139
  18.6 30.6 %collective-permute-start.14 = (bf16[256,1024]{1,0:T(8,128)(2,1)S(1)}, bf16[256,1024]{1,0:T(8,128)(2,1)S(1)}, u32[]{:S(2)}, u32[]{:S(2)}) collective-permute-start(bf16[256,1024]{1,0:T(8,128)(2,1)S(1)} %attend.1.refs_0_), channel_id=1, source_target_pairs={{8,16},{12,20},{16,8},{20,12},{9,17},{13,21},{17,9},{21,13},{10,18... | collective-permute-start | bytes 1572872 | tf_op jit(solution)/shard_map/ppermute | solution.py:143
  20.1 27.2 %collective-permute-start.5 = (bf16[256,1024]{1,0:T(8,128)(2,1)S(1)}, bf16[256,1024]{1,0:T(8,128)(2,1)S(1)}, u32[]{:S(2)}, u32[]{:S(2)}) collective-permute-start(bf16[256,1024]{1,0:T(8,128)(2,1)S(1)} %attend.1.refs_0_), channel_id=1, source_target_pairs={{0,8},{4,12},{8,0},{12,4},{16,24},{20,28},{24,16},{28,20},{1,9},{5... | collective-permute-start | bytes 1572872 | tf_op jit(solution)/shard_map/ppermute | solution.py:143
  40.9 15.2 %collective-permute-start.15 = (bf16[256,1024]{1,0:T(8,128)(2,1)S(1)}, bf16[256,1024]{1,0:T(8,128)(2,1)S(1)}, u32[]{:S(2)}, u32[]{:S(2)}) collective-permute-start(bf16[256,1024]{1,0:T(8,128)(2,1)S(1)} %collective-permute-done.10.refs_0_.refs_2_), channel_id=1, source_target_pairs={{8,0},{12,4},{16,24},{20,28},{9,1},{13,5},{17,25},{21,29},{10,2},{... | collective-permute-start | bytes 1572872 | tf_op jit(solution)/shard_map/ppermute | solution.py:143
  42.3 5.0 %collective-permute-start.4 = (bf16[64,1024]{1,0:T(8,128)(2,1)S(1)}, bf16[64,1024]{1,0:T(8,128)(2,1)S(1)}, u32[]{:S(2)}, u32[]{:S(2)}) collective-permute-start(bf16[64,1024]{1,0:T(8,128)(2,1)S(1)} %slice.155), channel_id=1, source_target_pairs={{0,2},{1,3},{2,0},{3,1},{4,6},{5,7},{6,4},{7,5},{8,10},{9,11},{10,... | collective-permute-start | bytes 393224 | tf_op jit(solution)/shard_map/ppermute | solution.py:154
  47.3 11.9 %collective-permute-start.11 = (bf16[128,1536]{1,0:T(8,128)(2,1)S(1)}, bf16[128,1536]{1,0:T(8,128)(2,1)S(1)}, u32[]{:S(2)}, u32[]{:S(2)}) collective-permute-start(bf16[128,1536]{1,0:T(8,128)(2,1)S(1)} %get-tuple-element.26), channel_id=1, source_target_pairs={{0,1},{1,0},{2,3},{3,2},{4,5},{5,4},{6,7},{7,6},{8,9},{9,8},{10,11... | collective-permute-start | bytes 1179656 | tf_op jit(solution)/shard_map/ppermute | solution.py:154
  48.6 13.0 %collective-permute-start.7 = (bf16[128,2048]{1,0:T(8,128)(2,1)S(1)}, bf16[128,2048]{1,0:T(8,128)(2,1)S(1)}, u32[]{:S(2)}, u32[]{:S(2)}) collective-permute-start(bf16[128,2048]{1,0:T(8,128)(2,1)S(1)} %get-tuple-element.24), channel_id=1, source_target_pairs={{0,1},{1,0},{2,3},{3,2},{4,5},{5,4},{6,7},{7,6},{8,9},{9,8},{10,11... | collective-permute-start | bytes 1572872 | tf_op jit(solution)/shard_map/ppermute | solution.py:154
  57.6 5.4 %collective-permute-start.20 = (bf16[128,2048]{1,0:T(8,128)(2,1)S(1)}, bf16[128,2048]{1,0:T(8,128)(2,1)S(1)}, u32[]{:S(2)}, u32[]{:S(2)}) collective-permute-start(bf16[128,2048]{1,0:T(8,128)(2,1)S(1)} %get-tuple-element.31), channel_id=1, source_target_pairs={{0,1},{1,0},{2,3},{3,2},{4,5},{5,4},{6,7},{7,6},{8,9},{9,8},{10,11... | collective-permute-start | bytes 1572872 | tf_op jit(solution)/shard_map/ppermute | solution.py:154
  58.7 1.9 %collective-permute-start.16 = (bf16[128,1536]{1,0:T(8,128)(2,1)S(1)}, bf16[128,1536]{1,0:T(8,128)(2,1)S(1)}, u32[]{:S(2)}, u32[]{:S(2)}) collective-permute-start(bf16[128,1536]{1,0:T(8,128)(2,1)S(1)} %get-tuple-element.28), channel_id=1, source_target_pairs={{0,1},{1,0},{2,3},{3,2},{4,5},{5,4},{6,7},{7,6},{8,9},{9,8},{10,11... | collective-permute-start | bytes 1179656 | tf_op jit(solution)/shard_map/ppermute | solution.py:154
  59.3 7.8 %collective-permute-start.12 = (bf16[64,1536]{1,0:T(8,128)(2,1)S(1)}, bf16[64,1536]{1,0:T(8,128)(2,1)S(1)}, u32[]{:S(2)}, u32[]{:S(2)}) collective-permute-start(bf16[64,1536]{1,0:T(8,128)(2,1)S(1)} %slice.154), channel_id=1, source_target_pairs={{0,2},{1,3},{2,0},{3,1},{4,6},{5,7},{6,4},{7,5},{8,10},{9,11},{10,... | collective-permute-start | bytes 589832 | tf_op jit(solution)/shard_map/ppermute | solution.py:154
  60.7 10.7 %collective-permute-start.17 = (bf16[64,1536]{1,0:T(8,128)(2,1)S(1)}, bf16[64,1536]{1,0:T(8,128)(2,1)S(1)}, u32[]{:S(2)}, u32[]{:S(2)}) collective-permute-start(bf16[64,1536]{1,0:T(8,128)(2,1)S(1)} %slice.153), channel_id=1, source_target_pairs={{0,2},{1,3},{2,0},{3,1},{4,6},{5,7},{6,4},{7,5},{8,10},{9,11},{10,... | collective-permute-start | bytes 589832 | tf_op jit(solution)/shard_map/ppermute | solution.py:154
  61.8 15.2 %collective-permute-start.8 = (bf16[64,2048]{1,0:T(8,128)(2,1)S(1)}, bf16[64,2048]{1,0:T(8,128)(2,1)S(1)}, u32[]{:S(2)}, u32[]{:S(2)}) collective-permute-start(bf16[64,2048]{1,0:T(8,128)(2,1)S(1)} %slice.152), channel_id=1, source_target_pairs={{0,2},{1,3},{2,0},{3,1},{4,6},{5,7},{6,4},{7,5},{8,10},{9,11},{10,... | collective-permute-start | bytes 786440 | tf_op jit(solution)/shard_map/ppermute | solution.py:154
  63.2 18.5 %collective-permute-start.21 = (bf16[64,2048]{1,0:T(8,128)(2,1)S(1)}, bf16[64,2048]{1,0:T(8,128)(2,1)S(1)}, u32[]{:S(2)}, u32[]{:S(2)}) collective-permute-start(bf16[64,2048]{1,0:T(8,128)(2,1)S(1)} %slice.151), channel_id=1, source_target_pairs={{0,2},{1,3},{2,0},{3,1},{4,6},{5,7},{6,4},{7,5},{8,10},{9,11},{10,... | collective-permute-start | bytes 786440 | tf_op jit(solution)/shard_map/ppermute | solution.py:154
  67.2 18.8 %collective-permute-start.13 = (bf16[64,1536]{1,0:T(8,128)(2,1)S(1)}, bf16[64,1536]{1,0:T(8,128)(2,1)S(1)}, u32[]{:S(2)}, u32[]{:S(2)}) collective-permute-start(bf16[64,1536]{1,0:T(8,128)(2,1)S(1)} %fusion.1), channel_id=1, source_target_pairs={{0,16},{4,20},{8,24},{12,28},{16,0},{20,4},{24,8},{28,12},{1,17},{... | collective-permute-start | bytes 589832 | tf_op jit(solution)/shard_map/ppermute | solution.py:143
  71.4 14.8 %collective-permute-start.18 = (bf16[64,1536]{1,0:T(8,128)(2,1)S(1)}, bf16[64,1536]{1,0:T(8,128)(2,1)S(1)}, u32[]{:S(2)}, u32[]{:S(2)}) collective-permute-start(bf16[64,1536]{1,0:T(8,128)(2,1)S(1)} %fusion), channel_id=1, source_target_pairs={{0,24},{4,28},{8,16},{12,20},{16,8},{20,12},{24,0},{28,4},{1,25},{... | collective-permute-start | bytes 589832 | tf_op jit(solution)/shard_map/ppermute | solution.py:143
  77.0 15.1 %collective-permute-start.9 = (bf16[64,1536]{1,0:T(8,128)(2,1)S(1)}, bf16[64,1536]{1,0:T(8,128)(2,1)S(1)}, u32[]{:S(2)}, u32[]{:S(2)}) collective-permute-start(bf16[64,1536]{1,0:T(8,128)(2,1)S(1)} %fusion.2), channel_id=1, source_target_pairs={{0,8},{4,12},{8,0},{12,4},{16,24},{20,28},{24,16},{28,20},{1,9},{5... | collective-permute-start | bytes 589832 | tf_op jit(solution)/shard_map/ppermute | solution.py:143
  81.8 6.3 %collective-permute-start.22 = (bf16[64,512]{1,0:T(8,128)(2,1)S(1)}, bf16[64,512]{1,0:T(8,128)(2,1)S(1)}, u32[]{:S(2)}, u32[]{:S(2)}) collective-permute-start(bf16[64,512]{1,0:T(8,128)(2,1)S(1)} %get-tuple-element.34), channel_id=1, source_target_pairs={{0,8},{4,12},{8,0},{12,4},{16,24},{20,28},{24,16},{28,20},{1,9},{5... | collective-permute-start | bytes 196616 | tf_op jit(solution)/shard_map/ppermute | solution.py:143
  81.8 8.3 %collective-permute-start.23 = (bf16[64,512]{1,0:T(8,128)(2,1)S(1)}, bf16[64,512]{1,0:T(8,128)(2,1)S(1)}, u32[]{:S(2)}, u32[]{:S(2)}) collective-permute-start(bf16[64,512]{1,0:T(8,128)(2,1)S(1)} %get-tuple-element.33), channel_id=1, source_target_pairs={{0,16},{4,20},{8,24},{12,28},{16,0},{20,4},{24,8},{28,12},{1,17},{... | collective-permute-start | bytes 196616 | tf_op jit(solution)/shard_map/ppermute | solution.py:143
  86.0 6.1 %collective-permute-start.24 = (bf16[64,512]{1,0:T(8,128)(2,1)S(1)}, bf16[64,512]{1,0:T(8,128)(2,1)S(1)}, u32[]{:S(2)}, u32[]{:S(2)}) collective-permute-start(bf16[64,512]{1,0:T(8,128)(2,1)S(1)} %get-tuple-element.32), channel_id=1, source_target_pairs={{0,24},{4,28},{8,16},{12,20},{16,8},{20,12},{24,0},{28,4},{1,25},{... | collective-permute-start | bytes 196616 | tf_op jit(solution)/shard_map/ppermute | solution.py:143
  (7 other events, 78.8 us)
